TPU v7x, 32 devices: a whole 2x2x4 slice. The times are simulated.
32 devices in a mesh: grp: 2 (over x), dev: 16 (over z, y, core).
Axes of the slice: x: 2, y: 2, z: 4, core: 2. Of those that a mesh axis runs over, the one named last changes fastest.
Arguments:
- voltages: int32 [512, 137216], P('dev', 'grp'), may hold values from -2147483648 to 2147483646
- block_order: int32 [10], replicated, may hold values from 0 to 9, each once
Outputs:
- visibilities: float32 [10, 2, 2, 1024, 128, 128], P('grp', None, None, 'dev')
Inputs may be any that keep to these rules, and one draw needn't show every extreme that they name: `block_order`: a permutation of the block pair numbers.
All inputs are finite; a program needn't handle non-finite values.
Results may differ from a plain program's by a relative error of at most 0.0058.
Values may be sent and summed in bfloat16 or wider, within the bound.
No kernel may reach another device: no remote copies, remote signals or barrier semaphores. Data moves between devices by JAX's collectives and lax.ppermute only.
A program may use at most 320 MiB of HBM per device.

v0:
```python
import jax
import jax.numpy as jnp
import numpy as np
from jax import lax
from jax.sharding import PartitionSpec as P

A = 512
FREQ_CHANNELS = 1024
FILTER_TAPS = 4
BLOCK_FRAMES = 64
INTEG_PERIODS = 2
BLOCK = 128


def unpack_packed_words(words):
    pieces = []
    for byte in range(4):
        raw = jnp.bitwise_and(jnp.right_shift(words, 8 * byte), 255)
        pieces.append((raw - 128).astype(jnp.float32) / 64.0)
    return jnp.concatenate(pieces, axis=-1)


def prototype():
    length = 2 * FREQ_CHANNELS
    position = jnp.arange(FILTER_TAPS * length, dtype=jnp.float32) + 0.5
    window = 0.5 - 0.5 * jnp.cos(2.0 * jnp.pi * position / (length * FILTER_TAPS))
    return jnp.sinc(position / length - FILTER_TAPS / 2.0) * window


def dft_table():
    length = 2 * FREQ_CHANNELS
    index = (
        jnp.arange(length, dtype=jnp.int32)[:, None]
        * jnp.arange(FREQ_CHANNELS, dtype=jnp.int32)[None, :]
    )
    angle = 2.0 * jnp.pi / length * (index % length).astype(jnp.float32)
    factor = length ** (-0.5)
    return jnp.stack([jnp.cos(angle) * factor, -jnp.sin(angle) * factor], axis=1).astype(
        jnp.bfloat16
    )


def filter_frames(voltage_samples, coeffs):
    weights = coeffs.reshape(FILTER_TAPS, 2 * FREQ_CHANNELS)
    total = voltage_samples[..., 0:BLOCK_FRAMES, :] * weights[0]
    for shift in range(1, FILTER_TAPS):
        total = total + voltage_samples[..., shift : shift + BLOCK_FRAMES, :] * weights[shift]
    return total.astype(jnp.bfloat16)


def pick(table, index):
    hits = jnp.arange(table.shape[0], dtype=jnp.int32) == index
    return jnp.sum(jnp.where(hits, table, 0)).astype(jnp.int32)


def twist_parts(data):
    width = data.shape[3]
    split = data.reshape(data.shape[:3] + (width // (2 * BLOCK_FRAMES), 2, BLOCK_FRAMES))
    return jnp.stack([split[..., 1, :], -split[..., 0, :]], axis=-2).reshape(data.shape)


def block_gram(data, twisted, slots, block_order, factor):
    upper_rows, upper_cols = np.triu_indices(A // BLOCK)
    pair_rows = jnp.asarray(upper_rows.astype(np.int32))
    pair_cols = jnp.asarray(upper_cols.astype(np.int32))

    def one_slot(slot):
        entry = pick(block_order, slot)
        row = pick(pair_rows, entry) * BLOCK
        col = pick(pair_cols, entry) * BLOCK
        left = lax.dynamic_slice_in_dim(data, row, BLOCK, 2)
        left_twist = lax.dynamic_slice_in_dim(twisted, row, BLOCK, 2)
        right = lax.dynamic_slice_in_dim(data, col, BLOCK, 2)
        real = jnp.einsum("ciak,cibk->icab", left, right, preferred_element_type=jnp.float32)
        imag = jnp.einsum("ciak,cibk->icab", left_twist, right, preferred_element_type=jnp.float32)
        return jnp.stack([real, imag], axis=1) * factor

    return lax.map(one_slot, slots)


def on_device(voltages, block_order):
    antennas_per_device = voltages.shape[0]
    groups = lax.axis_size("grp")
    factor = 1.0 / (groups * BLOCK_FRAMES)
    pair_count = A // BLOCK * (A // BLOCK + 1) // 2
    owned_count = pair_count // groups
    coeffs = prototype()
    table = dft_table()
    voltage_samples = unpack_packed_words(
        voltages.reshape(antennas_per_device, INTEG_PERIODS, -1)
    ).reshape(antennas_per_device, INTEG_PERIODS, BLOCK_FRAMES + FILTER_TAPS - 1, 2 * FREQ_CHANNELS)
    filtered = filter_frames(voltage_samples, coeffs)
    channel_spectra = jnp.einsum(
        "aifn,nrc->ciarf", filtered, table, preferred_element_type=jnp.float32
    )
    channel_spectra = channel_spectra.astype(jnp.bfloat16).reshape(
        FREQ_CHANNELS, INTEG_PERIODS, antennas_per_device, 2 * BLOCK_FRAMES
    )
    data = lax.all_to_all(channel_spectra, "dev", split_axis=0, concat_axis=2, tiled=True)
    twisted = twist_parts(data)
    owned = lax.axis_index("grp") * owned_count + jnp.arange(owned_count, dtype=jnp.int32)
    return block_gram(
        lax.all_gather(data, "grp", axis=3, tiled=True),
        lax.all_gather(twisted, "grp", axis=3, tiled=True),
        owned,
        block_order,
        factor,
    )


def solution(mesh):
    in_specs = (P("dev", "grp"), P())
    out_specs = P("grp", None, None, "dev", None, None)
    return jax.shard_map(
        on_device, mesh=mesh, in_specs=in_specs, out_specs=out_specs, check_vma=False
    )
```

profile of v0, /device:TPU:0, one launch (start us, length us, event | category | flops | bytes accessed | tf_op | source)
XLA Modules:
  0.0 1594.6 jit_solution(16311196921479738233)
XLA Ops:
  6.7 35.2 %multiply_convert_fusion = (bf16[2048,1,1024]{2,0,1:T(8,128)(2,1)}, bf16[2048,1,1024]{2,0,1:T(8,128)(2,1)}) fusion(), kind=kLoop, calls=%fused_computation.51 | loop fusion | flops 39845888 | bytes 8388608 | tf_op jit(solution)/shard_map/convert.1
  41.9 15.4 convert_multiply_fusion.3
  64.0 12.1 copy_bitcast_fusion.2
  76.1 28.5 %pad_maximum_fusion = f32[32,2,137216]{2,0,1:T(8,128)} fusion(f32[32,2,34304]{2,0,1:T(8,128)S(1)} %get-tuple-element.113, f32[32,2,34304]{2,0,1:T(8,128)S(1)} %get-tuple-element.114, f32[32,2,34304]{2,0,1:T(8,128)} %get-tuple-element.115, f32[32,2,34304]{2,0,1:T(8,128)} %get-tuple-element.116), kind=kLoop, calls=%fused_computation.19 | loop fusion | flops 26345472 | bytes 70254592 | tf_op jit(solution)/shard_map/concatenate | solution.py:20
  104.6 42.1 %reshape.164 = f32[32,2,67,2048]{3,2,0,1:T(8,128)} reshape(f32[32,2,137216]{2,0,1:T(8,128)} %pad_maximum_fusion) | data formatting | bytes 70254592 | tf_op jit(solution)/shard_map/reshape | solution.py:91
  146.7 59.8 %convert_bitcast_fusion = bf16[1024,2,32,2,64]{0,4,1,2,3:T(8,128)(2,1)} fusion(bf16[2048,1,1024]{2,0,1:T(8,128)(2,1)} %get-tuple-element.117, bf16[2048,1,1024]{2,0,1:T(8,128)(2,1)} %get-tuple-element.118, f32[32,2,67,2048]{3,2,0,1:T(8,128)} %reshape.164, f32[2048]{0:T(1024)S(1)} %get-tuple-element.110, f32[2048]{0:T(1024)S(1)} %get-tuple-element.111, ...), kind=kOutput, calls=%fused_computation.33 | convolution fusion | flops 34452013056 | bytes 159416320 | tf_op jit(solution)/shard_map/aifn,nrc->ciarf/dot_general | solution.py:93
  206.6 14.1 copy.35
  220.7 23.8 %copy.36 = bf16[1024,2,32,128]{3,2,1,0:T(8,128)(2,1)} copy(bf16[1024,2,32,128]{0,3,2,1:T(8,128)(2,1)} %bitcast.55) | data formatting | bytes 33554432 | tf_op jit(solution)/shard_map/reshape | solution.py:96
  244.5 369.3 %all_to_all.18 = bf16[1024,2,32,128]{3,2,1,0:T(8,128)(2,1)S(1)} all-to-all(bf16[1024,2,32,128]{3,2,1,0:T(8,128)(2,1)} %copy.36), channel_id=1, replica_groups=mesh['grp'=2,'dev'=16] {'dev'}, dimensions={0} | all-to-all | bytes 33554432 | tf_op jit(solution)/shard_map/all_to_all | solution.py:99
  621.6 54.9 %reshape.166 = bf16[64,2,512,1,2,64]{5,4,2,1,0,3:T(2,128)(2,1)} reshape(bf16[64,2,16,32,128]{4,3,2,1,0:T(8,128)(2,1)} %copy.37) | data formatting | bytes 33554432 | tf_op jit(solution)/shard_map/reshape | solution.py:58
  676.5 66.8 %fusion.52 = (bf16[64,2,512,1,1,64]{5,4,2,1,0,3:T(2,128)(2,1)}, bf16[64,2,512,1,1,64]{5,4,2,1,0,3:T(2,128)(2,1)}) fusion(bf16[64,2,512,1,2,64]{5,4,2,1,0,3:T(2,128)(2,1)} %reshape.166), kind=kLoop, calls=%fused_computation.82 | loop fusion | flops 4194304 | bytes 33554432 | tf_op jit(solution)/shard_map/slice | solution.py:59
  743.3 92.7 %pad_maximum_fusion.1 = bf16[64,2,512,1,2,64]{5,4,2,1,0,3:T(2,128)(2,1)} fusion(bf16[64,2,512,1,1,64]{5,4,2,1,0,3:T(2,128)(2,1)} %get-tuple-element.104, bf16[64,2,512,1,1,64]{5,4,2,1,0,3:T(2,128)(2,1)} %get-tuple-element.103), kind=kLoop, calls=%fused_computation.29 | loop fusion | flops 33554432 | bytes 33554432 | tf_op jit(solution)/shard_map/stack | solution.py:59
  836.0 65.5 %copy.39 = bf16[64,2,512,1,2,64]{2,5,4,1,0,3:T(8,128)(2,1)} copy(bf16[64,2,512,1,2,64]{5,4,2,1,0,3:T(2,128)(2,1)} %pad_maximum_fusion.1) | data formatting | bytes 33554432 | tf_op jit(solution)/shard_map/stack | solution.py:59
  901.6 110.5 %all-gather.3.cloned.1.call-done = bf16[64,2,512,256]{3,2,1,0:T(8,128)(2,1)} async-done(((bf16[64,2,512,128]{3,2,1,0:T(8,128)(2,1)}), bf16[64,2,512,256]{3,2,1,0:T(8,128)(2,1)}) %all-gather.3.cloned.1.call-update) | async-done | bytes 33554448 | tf_op jit(solution)/shard_map/all_gather | solution.py:103
  1012.1 28.7 %copy.40 = bf16[64,2,512,256]{3,2,0,1:T(8,128)(2,1)} copy(bf16[64,2,512,256]{3,2,1,0:T(8,128)(2,1)} %all-gather.3.cloned.1.call-done) | data formatting | bytes 67108864
  1040.8 361.4 %all-gather.5.cloned.1.call-done = bf16[64,2,512,256]{2,3,1,0:T(8,128)(2,1)} async-done(((bf16[64,2,512,128]{2,3,1,0:T(8,128)(2,1)}), bf16[64,2,512,256]{2,3,1,0:T(8,128)(2,1)}) %all-gather.5.cloned.1.call-update) | async-done | bytes 33554448 | tf_op jit(solution)/shard_map/all_gather | solution.py:104
  1402.2 185.6 %while.11 = (s32[]{:T(128)}, f32[5,2,2,64,128,128]{5,4,3,2,1,0:T(8,128)}, s32[5]{0:T(128)S(1)}, s32[10]{0:T(128)S(1)}, bf16[64,2,512,256]{3,2,0,1:T(8,128)(2,1)}...) while((s32[]{:T(128)}, ...), condition=%wide.region_4.5_spmd.clone, body=%wide.region_0.4_spmd.sunk.clone.sunk | while | flops 2155872256 | bytes 117441424 | solution.py:78
  1406.7 11.5 fusion.77
  1418.2 9.7 fusion.76
  1429.5 9.9 copy_dynamic-update-slice_fusion.2
  1443.9 11.5 fusion.77
  1455.3 9.7 fusion.76
  1466.6 9.9 copy_dynamic-update-slice_fusion.2
  1481.0 11.5 fusion.77
  1492.4 9.7 fusion.76
  1503.7 9.9 copy_dynamic-update-slice_fusion.2
  1518.1 11.5 fusion.77
  1529.5 9.7 fusion.76
  1540.8 9.9 copy_dynamic-update-slice_fusion.2
  1555.2 11.5 fusion.77
  1566.6 9.7 fusion.76
  1577.9 9.9 copy_dynamic-update-slice_fusion.2
  (41 shorter events, 38.8 us)
Async XLA Ops:
  6.5 1005.6 %all-gather.3.cloned.1.call-start = ((), (), s32[]{:S(2)}) async-start(), calls=%async_computation.1 | async-start | bytes 50331648 | tf_op jit(solution)/shard_map/all_gather | solution.py:103
  621.6 780.7 %all-gather.5.cloned.1.call-start = ((), (), s32[]{:S(2)}) async-start(), calls=%async_computation.2 | async-start | bytes 50331648 | tf_op jit(solution)/shard_map/all_gather | solution.py:104
  901.6 500.6 %copy-start.1 = (s32[10]{0:T(128)S(1)}, s32[10]{0:T(128)}, u32[]{:S(2)}) copy-start(s32[10]{0:T(128)} %constant.119.clone..sunk.2) | copy-start | bytes 124
  901.6 500.6 %copy-start.2 = (s32[10]{0:T(128)S(1)}, s32[10]{0:T(128)}, u32[]{:S(2)}) copy-start(s32[10]{0:T(128)} %constant.120.clone..sunk.2) | copy-start | bytes 124
  901.6 500.6 %copy-start.3 = (s32[10]{0:T(128)S(1)}, s32[10]{0:T(128)}, u32[]{:S(2)}) copy-start(s32[10]{0:T(128)} %param.7) | copy-start | bytes 124
  1418.2 11.3 copy-start
  1455.3 11.3 copy-start
  1492.4 11.3 copy-start
  1529.5 11.3 copy-start
  1566.6 11.3 copy-start
Sparse Core Ops, SparseCore 0:
  621.7 390.3 all-gather.2
  1013.7 388.5 all-gather.4
where the time goes:
time: 1600 us; the launch traced here: 1590 us
  waiting for transfers between devices  472 us (30%)
  blocking collectives  369 us (23%)
  other arithmetic  301 us (19%)
  local copies, waits for them, and re-layouts  267 us (17%)
  matrix products  166 us (10%)
    all_to_all x1, blocking collectives, on_device(): lax.all_to_all(channel_spectra, 'dev', split_axis=0, concat_axis=2, tiled...  369 us
    all_gather x1, waiting for transfers between devices, on_device(): lax.all_gather(twisted, 'grp', axis=3, tiled=True)  361 us
    all_gather x1, waiting for transfers between devices, on_device(): lax.all_gather(data, 'grp', axis=3, tiled=True)  110 us
    another operation x1, other arithmetic, twist_parts(): jnp.stack([split[..., 1, :], -split[..., 0, :]], axis=-2)  92.7 us
    slice x1, other arithmetic, twist_parts(): split[..., 1, :]  66.8 us
    another operation x1, local copies, waits for them, and re-layouts, twist_parts(): jnp.stack([split[..., 1, :], -split[..., 0, :]], axis=-2)  65.5 us
    dot_general x1, matrix products, on_device(): jnp.einsum('aifn,nrc->ciarf', filtered, table, preferred_element_type=jnp...  59.8 us
    dot_general x5, matrix products, one_slot(): jnp.einsum('ciak,cibk->icab', left, right, preferred_element_type=jnp.flo...  57.3 us
  transfers between devices with their start and end apart: 2, of which 2 were waited for; matrix products, arithmetic and copies ran while one was open for 19% of the time, Pallas kernels for 0%

commit v1 on v0

v1 whole, which is shorter than its diff:
```python
import functools

import jax
import jax.numpy as jnp
import numpy as np
from jax import lax
from jax.experimental import pallas as pl
from jax.experimental.pallas import tpu as pltpu
from jax.sharding import PartitionSpec as P

FREQ_CHANNELS = 1024
FILTER_TAPS = 4
BLOCK_FRAMES = 64
INTEG_PERIODS = 2
BLOCK = 128
LENGTH = 2 * FREQ_CHANNELS
QUARTER = LENGTH // 4
WORD_ROWS = BLOCK_FRAMES + FILTER_TAPS - 1
QUAD = 4
CHUNKS = 4


def prototype():
    position = jnp.arange(FILTER_TAPS * LENGTH, dtype=jnp.float32) + 0.5
    window = 0.5 - 0.5 * jnp.cos(2.0 * jnp.pi * position / (LENGTH * FILTER_TAPS))
    return jnp.sinc(position / LENGTH - FILTER_TAPS / 2.0) * window


def dft_rows(devices, chunks):
    channels = jnp.arange(FREQ_CHANNELS, dtype=jnp.int32)
    channels = channels.reshape(devices, chunks, -1).swapaxes(0, 1).reshape(-1)
    index = channels[:, None] * jnp.arange(LENGTH, dtype=jnp.int32)[None, :]
    angle = 2.0 * jnp.pi / LENGTH * (index % LENGTH).astype(jnp.float32)
    factor = LENGTH ** (-0.5)
    return jnp.stack([jnp.cos(angle) * factor, -jnp.sin(angle) * factor]).astype(jnp.bfloat16)


def spectra_kernel(words_ref, weights_ref, table_ref, *refs, group, chunks):
    outs = refs[:chunks]
    planes, filtered, scratch = refs[chunks:]
    for quad in range(group // QUAD):
        for part in range(QUAD):
            antenna = quad * QUAD + part
            for lane in range(QUARTER // 128):
                words = words_ref[antenna, 0, :, lane * 128 : (lane + 1) * 128]
                flipped = words ^ jnp.int32(-2139062144)
                for byte in range(4):
                    value = lax.shift_right_arithmetic(flipped << (24 - 8 * byte), 24)
                    planes[lane, byte * WORD_ROWS : (byte + 1) * WORD_ROWS, :] = value.astype(jnp.float32)
            for lane in range(QUARTER // 128):
                for m in range(4):
                    start = m * QUARTER + lane * 128
                    total = None
                    for tap in range(FILTER_TAPS):
                        piece = planes[lane, pl.ds(4 * tap + m, BLOCK_FRAMES, stride=4), :]
                        term = piece * weights_ref[tap : tap + 1, start : start + 128]
                        total = term if total is None else total + term
                    filtered[part * BLOCK_FRAMES : (part + 1) * BLOCK_FRAMES, start : start + 128] = total.astype(
                        jnp.bfloat16
                    )
        frames = filtered[...]
        rows = FREQ_CHANNELS // chunks
        low = lax.broadcasted_iota(jnp.int32, (rows, 128), 1) < BLOCK_FRAMES
        for chunk in range(chunks):
            both = []
            for r in range(2):
                both.append(
                    lax.dot_general(
                        table_ref[r, chunk * rows : (chunk + 1) * rows, :],
                        frames,
                        (((1,), (1,)), ((), ())),
                        preferred_element_type=jnp.float32,
                    )
                )
            for pair in range(QUAD // 2):
                real = both[0][:, pair * 128 : (pair + 1) * 128]
                imag = both[1][:, pair * 128 : (pair + 1) * 128]
                first = jnp.where(low, real, pltpu.roll(imag, 64, 1))
                second = jnp.where(low, pltpu.roll(real, 64, 1), imag)
                antenna = quad * QUAD + pair * 2
                base = chunk * rows * group
                scratch[pl.ds(base + antenna, rows, stride=group), :] = first
                scratch[pl.ds(base + antenna + 1, rows, stride=group), :] = second
    rows = FREQ_CHANNELS // chunks
    for chunk in range(chunks):
        piece = scratch[chunk * rows * group : (chunk + 1) * rows * group, :]
        outs[chunk][...] = piece.reshape(rows, group, 128).astype(jnp.bfloat16)


def make_spectra(words, weights, table, integ, chunks):
    antennas = words.shape[0]
    group = min(antennas, 16)
    rows = FREQ_CHANNELS // chunks
    return pl.pallas_call(
        functools.partial(spectra_kernel, group=group, chunks=chunks),
        grid=(antennas // group,),
        in_specs=[
            pl.BlockSpec((group, 1, WORD_ROWS, QUARTER), lambda s: (s, integ, 0, 0)),
            pl.BlockSpec((FILTER_TAPS, LENGTH), lambda s: (0, 0)),
            pl.BlockSpec((2, FREQ_CHANNELS, LENGTH), lambda s: (0, 0, 0)),
        ],
        out_specs=[pl.BlockSpec((rows, group, 128), lambda s: (0, s, 0)) for _ in range(chunks)],
        out_shape=[jax.ShapeDtypeStruct((rows, antennas, 128), jnp.bfloat16) for _ in range(chunks)],
        scratch_shapes=[
            pltpu.VMEM((QUARTER // 128, 4 * WORD_ROWS, 128), jnp.float32),
            pltpu.VMEM((QUAD * BLOCK_FRAMES, LENGTH), jnp.bfloat16),
            pltpu.VMEM((FREQ_CHANNELS * group, 128), jnp.float32),
        ],
        name=f"spectra_{integ}",
    )(words, weights, table)


def gram_kernel(picks_ref, *refs, sources, per_block, factor, owned, batch, aliased):
    data = refs[:sources]
    out_ref = refs[sources + (1 if aliased else 0)]
    low = lax.broadcasted_iota(jnp.int32, (BLOCK, 128), 1) < BLOCK_FRAMES
    for channel in range(batch):
        for slot in range(owned):
            row = picks_ref[slot]
            col = picks_ref[owned + slot]
            lefts, rights, twists = [], [], []
            for ref in data:
                left = ref[pl.ds(row * per_block, per_block), channel].reshape(BLOCK, 128)
                right = ref[pl.ds(col * per_block, per_block), channel].reshape(BLOCK, 128)
                turned = pltpu.roll(right.astype(jnp.float32), 64, 1)
                twists.append(jnp.where(low, -turned, turned).astype(jnp.bfloat16))
                lefts.append(left)
                rights.append(right)
            left = jnp.concatenate(lefts, axis=1)
            right = jnp.concatenate([jnp.concatenate(rights, axis=1), jnp.concatenate(twists, axis=1)], axis=0)
            both = lax.dot_general(
                left, right, (((1,), (1,)), ((), ())), preferred_element_type=jnp.float32
            ) * factor
            out_ref[slot, 0, 0, channel] = both[:, :BLOCK]
            out_ref[slot, 0, 1, channel] = both[:, BLOCK:]


def gram(picks, data, carry, integ, chunk, shape, factor):
    devices, count, antennas, _ = data[0].shape
    batch = min(count, 4)
    owned = shape[0]
    steps = count // batch
    aliased = carry is not None
    in_specs = [pl.BlockSpec((devices, batch, antennas, 128), lambda s, p: (0, s, 0, 0)) for _ in data]
    operands = [picks, *data]
    if aliased:
        in_specs.append(pl.BlockSpec(memory_space=pl.ANY))
        operands.append(carry)
    return pl.pallas_call(
        functools.partial(
            gram_kernel,
            sources=len(data),
            per_block=BLOCK // antennas,
            factor=factor,
            owned=owned,
            batch=batch,
            aliased=aliased,
        ),
        grid_spec=pltpu.PrefetchScalarGridSpec(
            num_scalar_prefetch=1,
            grid=(steps,),
            in_specs=in_specs,
            out_specs=pl.BlockSpec(
                (owned, 1, 2, batch, BLOCK, BLOCK), lambda s, p: (0, integ, 0, chunk * steps + s, 0, 0)
            ),
        ),
        out_shape=jax.ShapeDtypeStruct(shape, jnp.float32),
        input_output_aliases={len(operands) - 1: 0} if aliased else {},
        name=f"gram_{integ}_{chunk}",
    )(*operands)


def on_device(voltages, block_order):
    antennas = voltages.shape[0]
    groups = lax.axis_size("grp")
    devices = lax.axis_size("dev")
    blocks = antennas * devices // BLOCK
    owned_count = block_order.shape[0] // groups
    local = FREQ_CHANNELS // devices
    chunks = min(CHUNKS, local)
    words = voltages.reshape(antennas, INTEG_PERIODS, WORD_ROWS, QUARTER)
    weights = prototype().reshape(FILTER_TAPS, LENGTH) / 64.0
    table = dft_rows(devices, chunks)

    upper_rows, upper_cols = np.triu_indices(blocks)
    owned = lax.axis_index("grp") * owned_count + jnp.arange(owned_count, dtype=jnp.int32)
    entries = block_order[owned]
    picks = jnp.concatenate(
        [
            jnp.asarray(upper_rows.astype(np.int32))[entries],
            jnp.asarray(upper_cols.astype(np.int32))[entries],
        ]
    )
    factor = 1.0 / (groups * BLOCK_FRAMES)
    shape = (owned_count, INTEG_PERIODS, 2, local, BLOCK, BLOCK)
    pieces = []
    for integ in range(INTEG_PERIODS):
        pieces.extend(make_spectra(words, weights, table, integ, chunks))
    received = []
    for step, piece in enumerate(pieces):
        if step >= 2:
            piece, received[step - 2] = lax.optimization_barrier((piece, received[step - 2]))
        mine = lax.all_to_all(
            piece.reshape(devices, local // chunks, antennas, 128), "dev", split_axis=0, concat_axis=0, tiled=True
        )
        data = [mine]
        for shift in range(1, groups):
            ring = [(g, (g + shift) % groups) for g in range(groups)]
            data.append(lax.ppermute(mine, "grp", ring))
        received.append(data)
    out = None
    for step, data in enumerate(received):
        out = gram(picks, data, out, step // chunks, step % chunks, shape, factor)
    return out


def solution(mesh):
    in_specs = (P("dev", "grp"), P())
    out_specs = P("grp", None, None, "dev", None, None)
    return jax.shard_map(
        on_device, mesh=mesh, in_specs=in_specs, out_specs=out_specs, check_vma=False
    )
```

time: 1600 us -> 605 us (0.38)
  blocking collectives: 369 us -> 54.7 us
  other arithmetic: 301 us -> 46.3 us
  local copies, waits for them, and re-layouts: 267 us -> 15.3 us
  waiting for transfers between devices: 472 us -> 274 us
  matrix products: 166 us -> 0 us
  Pallas kernels: 0 us -> 153 us
  starting transfers between devices: 0.04 us -> 52.2 us
    all_gather x2 -> x0, waiting for transfers between devices: 472 us -> none  [the longest x1 361 us: on_device(): lax.all_gather(twisted, 'grp', axis=3, tiled=True)]
    all_to_all x1, blocking collectives: 369 us -> 54.7 us  [on_device(): lax.all_to_all(piece.reshape(devices, local // chunks, antennas, 128), 'd...]
    ppermute x0 -> x8, waiting for transfers between devices: none -> 234 us  [on_device(): data.append(lax.ppermute(mine, 'grp', ring))]
    dot_general x11 -> x0, matrix products: 166 us -> none  [the longest x1 59.8 us: on_device(): jnp.einsum('aifn,nrc->ciarf', filtered, table, preferred_element_type=jnp...]
    pallas_call x0 -> x10, Pallas kernels: none -> 153 us  [the longest x2 81.3 us: make_spectra(): pl.pallas_call(functools.partial(spectra_kernel, group=group, chunks=chun...]
    reshape x3 -> x2, local copies, waits for them, and re-layouts: 121 us -> 8.03 us  [the longest x1 7.96 us: on_device(): words = voltages.reshape(antennas, INTEG_PERIODS, WORD_ROWS, QUARTER)]
    another operation x2, other arithmetic: 128 us -> 44.7 us  [the longest x1 92.7 us: twist_parts(): jnp.stack([split[..., 1, :], -split[..., 0, :]], axis=-2)]
    slice x1 -> x0, other arithmetic: 66.8 us -> none  [twist_parts(): split[..., 1, :]]
  transfers between devices with their start and end apart: 2 -> 15, of which waited for: 2 -> 7; matrix products, arithmetic and copies ran while one was open for 19% -> 0% of each run, Pallas kernels for 0% -> 18%
where the time goes in v1:
time: 605 us; the launch traced here: 595 us
  waiting for transfers between devices  274 us (45%)
  Pallas kernels  153 us (25%)
  blocking collectives  54.7 us (9%)
  starting transfers between devices  52.2 us (9%)
  other arithmetic  46.3 us (8%)
  local copies, waits for them, and re-layouts  15.3 us (3%)
    ppermute x8, waiting for transfers between devices, on_device(): data.append(lax.ppermute(mine, 'grp', ring))  234 us
    pallas_call x2, Pallas kernels, make_spectra(): pl.pallas_call(functools.partial(spectra_kernel, group=group, chunks=chun...  81.3 us
    pallas_call x8, Pallas kernels, gram(): pl.pallas_call(functools.partial(gram_kernel, sources=len(data), per_bloc...  71.3 us
    all_to_all x1, blocking collectives, on_device(): lax.all_to_all(piece.reshape(devices, local // chunks, antennas, 128), 'd...  54.7 us
    all_to_all x7, starting transfers between devices, on_device(): lax.all_to_all(piece.reshape(devices, local // chunks, antennas, 128), 'd...  39.8 us
    all_to_all x7, waiting for transfers between devices, on_device(): lax.all_to_all(piece.reshape(devices, local // chunks, antennas, 128), 'd...  39.5 us
    another operation x1, other arithmetic  37.2 us
    ppermute x8, starting transfers between devices, on_device(): data.append(lax.ppermute(mine, 'grp', ring))  12.4 us
  transfers between devices with their start and end apart: 15, of which 7 were waited for; matrix products, arithmetic and copies ran while one was open for 0% of the time, Pallas kernels for 18%

profile of v1, /device:TPU:0, one launch (start us, length us, event | category | flops | bytes accessed | tf_op | source)
XLA Modules:
  0.0 595.1 jit_solution(11537787001954836170)
XLA Ops:
  1.0 37.2 %multiply_convert_fusion.1 = (bf16[1,1024,2048]{2,1,0:T(8,128)(2,1)}, bf16[1,1024,2048]{2,1,0:T(8,128)(2,1)}) fusion(s32[1024]{0:T(1024)S(1)} %reshape.224), kind=kLoop, calls=%fused_computation.11 | loop fusion | flops 39845888 | bytes 8392704 | tf_op jit(solution)/shard_map/convert
  38.3 8.0 %reshape.217.words_ref = s32[32,2,67,512]{3,2,1,0:T(8,128)} reshape(s32[32,68608]{1,0:T(8,128)} %param.4) | data formatting | bytes 17563648 | tf_op jit(solution)/shard_map/reshape | solution.py:181
  46.2 7.5 %pad_maximum_fusion.table_ref = bf16[2,1024,2048]{2,1,0:T(8,128)(2,1)} fusion(bf16[1,1024,2048]{2,1,0:T(8,128)(2,1)} %get-tuple-element.58, bf16[1,1024,2048]{2,1,0:T(8,128)(2,1)} %get-tuple-element.57), kind=kLoop, calls=%fused_computation.9 | loop fusion | flops 4194304 | bytes 16777216 | tf_op jit(solution)/shard_map/stack | solution.py:35
  53.7 36.2 %spectra_0.1 = (bf16[256,32,128]{2,1,0:T(8,128)(2,1)}, bf16[256,32,128]{2,1,0:T(8,128)(2,1)}, bf16[256,32,128]{2,1,0:T(8,128)(2,1)}, bf16[256,32,128]{2,1,0:T(8,128)(2,1)}) custom-call(s32[32,2,67,512]{3,2,1,0:T(8,128)} %reshape.217.words_ref, f32[4,2048]{1,0:T(4,128)} %fusion.12.weights_ref, bf16[2,1024,2048]{2,1,0:T(8,128)(2,1)} %pad_maximum_fusion.table_ref), custom_call_target="tpu_custom_call" | custom-call | tf_op jit(solution)/shard_map/spectra_0/pallas_call | solution.py:94
  90.0 54.7 %all_to_all.40.refs_0_ = bf16[16,16,32,128]{3,2,1,0:T(8,128)(2,1)} all-to-all(bf16[16,16,32,128]{3,2,1,0:T(8,128)(2,1)} %bitcast.21), channel_id=1, replica_groups=mesh['grp'=2,'dev'=16] {'dev'}, dimensions={0} | all-to-all | bytes 4194304 | tf_op jit(solution)/shard_map/all_to_all | solution.py:203
  144.6 5.1 all-to-all-start
  151.3 46.6 %collective-permute-done.4.refs_1_ = bf16[16,16,32,128]{3,2,1,0:T(8,128)(2,1)S(1)} collective-permute-done((bf16[16,16,32,128]{3,2,1,0:T(8,128)(2,1)}, bf16[16,16,32,128]{3,2,1,0:T(8,128)(2,1)S(1)}, u32[]{:S(2)}, u32[]{:S(2)}) %collective-permute-start.4) | collective-permute-done | bytes 2097184 | tf_op jit(solution)/shard_map/ppermute | solution.py:209
  199.3 5.8 all-to-all-start.5
  205.0 1.6 collective-permute-start
  206.6 46.3 %collective-permute-done.refs_1_ = bf16[16,16,32,128]{3,2,1,0:T(8,128)(2,1)S(1)} collective-permute-done((bf16[16,16,32,128]{3,2,1,0:T(8,128)(2,1)S(1)}, bf16[16,16,32,128]{3,2,1,0:T(8,128)(2,1)S(1)}, u32[]{:S(2)}, u32[]{:S(2)}) %collective-permute-start) | collective-permute-done | bytes 2097184 | tf_op jit(solution)/shard_map/ppermute | solution.py:209
  254.3 5.8 all-to-all-start.1
  261.6 45.0 %spectra_1.1 = (bf16[256,32,128]{2,1,0:T(8,128)(2,1)}, bf16[256,32,128]{2,1,0:T(8,128)(2,1)}, bf16[256,32,128]{2,1,0:T(8,128)(2,1)}, bf16[256,32,128]{2,1,0:T(8,128)(2,1)}) custom-call(s32[32,2,67,512]{3,2,1,0:T(8,128)} %reshape.217.words_ref, f32[4,2048]{1,0:T(4,128)} %fusion.12.weights_ref, bf16[2,1024,2048]{2,1,0:T(8,128)(2,1)} %pad_maximum_fusion.table_ref), custom_call_target="tpu_custom_call" | custom-call | tf_op jit(solution)/shard_map/spectra_1/pallas_call | solution.py:94
  306.6 1.6 collective-permute-done.5.refs_1_
  308.3 5.9 all-to-all-start.6
  315.7 46.6 %collective-permute-done.1.refs_1_ = bf16[16,16,32,128]{3,2,1,0:T(8,128)(2,1)S(1)} collective-permute-done((bf16[16,16,32,128]{3,2,1,0:T(8,128)(2,1)}, bf16[16,16,32,128]{3,2,1,0:T(8,128)(2,1)S(1)}, u32[]{:S(2)}, u32[]{:S(2)}) %collective-permute-start.1) | collective-permute-done | bytes 2097184 | tf_op jit(solution)/shard_map/ppermute | solution.py:209
  363.6 5.8 all-to-all-start.2
  369.4 1.6 collective-permute-start.6
  370.9 46.3 %collective-permute-done.6.refs_1_ = bf16[16,16,32,128]{3,2,1,0:T(8,128)(2,1)S(1)} collective-permute-done((bf16[16,16,32,128]{3,2,1,0:T(8,128)(2,1)S(1)}, bf16[16,16,32,128]{3,2,1,0:T(8,128)(2,1)S(1)}, u32[]{:S(2)}, u32[]{:S(2)}) %collective-permute-start.6) | collective-permute-done | bytes 2097184 | tf_op jit(solution)/shard_map/ppermute | solution.py:209
  418.7 5.8 all-to-all-start.7
  424.4 1.6 collective-permute-start.2
  426.0 46.7 %collective-permute-done.2.refs_1_ = bf16[16,16,32,128]{3,2,1,0:T(8,128)(2,1)} collective-permute-done((bf16[16,16,32,128]{3,2,1,0:T(8,128)(2,1)}, bf16[16,16,32,128]{3,2,1,0:T(8,128)(2,1)}, u32[]{:S(2)}, u32[]{:S(2)}) %collective-permute-start.2) | collective-permute-done | bytes 2097184 | tf_op jit(solution)/shard_map/ppermute | solution.py:209
  472.6 5.8 all-to-all-start.3
  478.4 1.6 collective-permute-start.7
  480.0 39.5 %all-to-all-done.3.refs_0_ = bf16[16,16,32,128]{3,2,1,0:T(8,128)(2,1)} async-done(((bf16[16,16,32,128]{3,2,1,0:T(8,128)(2,1)}), bf16[16,16,32,128]{3,2,1,0:T(8,128)(2,1)}, u32[]{:S(2)}, u32[]{:S(2)}) %all-to-all-start.3) | async-done | bytes 2097184 | tf_op jit(solution)/shard_map/all_to_all | solution.py:203
  523.6 8.9 %gram_0_0.1.refs_2_ = f32[5,2,2,64,128,128]{5,4,3,2,1,0:T(8,128)} custom-call(s32[10]{0:T(128)} %pad_add_fusion.picks_ref, bf16[16,16,32,128]{3,2,1,0:T(8,128)(2,1)} %all_to_all.40.refs_0_, bf16[16,16,32,128]{3,2,1,0:T(8,128)(2,1)} %copy-done.9), custom_call_target="tpu_custom_call" | custom-call | tf_op jit(solution)/shard_map/gram_0_0/pallas_call | solution.py:149
  532.4 8.9 %gram_0_1.1.refs_2_ = f32[5,2,2,64,128,128]{5,4,3,2,1,0:T(8,128)} custom-call(s32[10]{0:T(128)} %pad_add_fusion.picks_ref, bf16[16,16,32,128]{3,2,1,0:T(8,128)(2,1)} %copy-done.4, bf16[16,16,32,128]{3,2,1,0:T(8,128)(2,1)} %copy-done.6, f32[5,2,2,64,128,128]{5,4,3,2,1,0:T(8,128)} %gram_0_0.1.refs_2_), custom_call_target="tpu_custom_call", output_to_operand_aliasing={{}: (3, {})} | custom-call | tf_op jit(solution)/shard_map/gram_0_1/pallas_call | solution.py:149
  541.4 8.9 %gram_0_2.1.refs_2_ = f32[5,2,2,64,128,128]{5,4,3,2,1,0:T(8,128)} custom-call(s32[10]{0:T(128)} %pad_add_fusion.picks_ref, bf16[16,16,32,128]{3,2,1,0:T(8,128)(2,1)} %all-to-all-done.5.refs_0_, bf16[16,16,32,128]{3,2,1,0:T(8,128)(2,1)} %collective-permute-done.5.refs_1_, f32[5,2,2,64,128,128]{5,4,3,2,1,0:T(8,128)} %gram_0_1.1.refs_2_), custom_call_target="tpu_custom_call", output_to_operand_aliasing={{}: (3, {})} | custom-call | tf_op jit(solution)/shard_map/gram_0_2/pallas_call | solution.py:149
  550.3 8.9 %gram_0_3.1.refs_2_ = f32[5,2,2,64,128,128]{5,4,3,2,1,0:T(8,128)} custom-call(s32[10]{0:T(128)} %pad_add_fusion.picks_ref, bf16[16,16,32,128]{3,2,1,0:T(8,128)(2,1)} %all-to-all-done.1.refs_0_, bf16[16,16,32,128]{3,2,1,0:T(8,128)(2,1)} %copy-done.7, f32[5,2,2,64,128,128]{5,4,3,2,1,0:T(8,128)} %gram_0_2.1.refs_2_), custom_call_target="tpu_custom_call", output_to_operand_aliasing={{}: (3, {})} | custom-call | tf_op jit(solution)/shard_map/gram_0_3/pallas_call | solution.py:149
  559.2 8.9 %gram_1_0.1.refs_2_ = f32[5,2,2,64,128,128]{5,4,3,2,1,0:T(8,128)} custom-call(s32[10]{0:T(128)} %pad_add_fusion.picks_ref, bf16[16,16,32,128]{3,2,1,0:T(8,128)(2,1)} %copy-done.5, bf16[16,16,32,128]{3,2,1,0:T(8,128)(2,1)} %copy-done.8, f32[5,2,2,64,128,128]{5,4,3,2,1,0:T(8,128)} %gram_0_3.1.refs_2_), custom_call_target="tpu_custom_call", output_to_operand_aliasing={{}: (3, {})} | custom-call | tf_op jit(solution)/shard_map/gram_1_0/pallas_call | solution.py:149
  568.1 8.9 %gram_1_1.1.refs_2_ = f32[5,2,2,64,128,128]{5,4,3,2,1,0:T(8,128)} custom-call(s32[10]{0:T(128)} %pad_add_fusion.picks_ref, bf16[16,16,32,128]{3,2,1,0:T(8,128)(2,1)} %all-to-all-done.2.refs_0_, bf16[16,16,32,128]{3,2,1,0:T(8,128)(2,1)} %collective-permute-done.2.refs_1_, f32[5,2,2,64,128,128]{5,4,3,2,1,0:T(8,128)} %gram_1_0.1.refs_2_), custom_call_target="tpu_custom_call", output_to_operand_aliasing={{}: (3, {})} | custom-call | tf_op jit(solution)/shard_map/gram_1_1/pallas_call | solution.py:149
  577.0 8.9 %gram_1_2.1.refs_2_ = f32[5,2,2,64,128,128]{5,4,3,2,1,0:T(8,128)} custom-call(s32[10]{0:T(128)} %pad_add_fusion.picks_ref, bf16[16,16,32,128]{3,2,1,0:T(8,128)(2,1)} %all-to-all-done.7.refs_0_, bf16[16,16,32,128]{3,2,1,0:T(8,128)(2,1)} %collective-permute-done.7.refs_1_, f32[5,2,2,64,128,128]{5,4,3,2,1,0:T(8,128)} %gram_1_1.1.refs_2_), custom_call_target="tpu_custom_call", output_to_operand_aliasing={{}: (3, {})} | custom-call | tf_op jit(solution)/shard_map/gram_1_2/pallas_call | solution.py:149
  585.9 9.0 %gram_1_3.1 = f32[5,2,2,64,128,128]{5,4,3,2,1,0:T(8,128)} custom-call(s32[10]{0:T(128)} %pad_add_fusion.picks_ref, bf16[16,16,32,128]{3,2,1,0:T(8,128)(2,1)} %all-to-all-done.3.refs_0_, bf16[16,16,32,128]{3,2,1,0:T(8,128)(2,1)} %collective-permute-done.3.refs_1_, f32[5,2,2,64,128,128]{5,4,3,2,1,0:T(8,128)} %gram_1_2.1.refs_2_), custom_call_target="tpu_custom_call", output_to_operand_aliasing={{}: (3, {})} | custom-call | tf_op jit(solution)/shard_map/gram_1_3/pallas_call | solution.py:149
  (43 shorter events, 15.2 us)
Async XLA Ops:
  0.0 521.0 %copy-start = (s32[10]{0:T(128)S(1)}, s32[10]{0:T(128)}, u32[]{:S(2)}) copy-start(s32[10]{0:T(128)} %param.5) | copy-start | bytes 124
  144.6 54.6 %all-to-all-start = ((bf16[16,16,32,128]{3,2,1,0:T(8,128)(2,1)}), bf16[16,16,32,128]{3,2,1,0:T(8,128)(2,1)S(1)}, u32[]{:S(2)}, u32[]{:S(2)}) async-start(bf16[16,16,32,128]{3,2,1,0:T(8,128)(2,1)} %bitcast.20), calls=%async_computation | async-start | bytes 4194304 | tf_op jit(solution)/shard_map/all_to_all | solution.py:203
  149.8 48.2 %collective-permute-start.4 = (bf16[16,16,32,128]{3,2,1,0:T(8,128)(2,1)}, bf16[16,16,32,128]{3,2,1,0:T(8,128)(2,1)S(1)}, u32[]{:S(2)}, u32[]{:S(2)}) collective-permute-start(bf16[16,16,32,128]{3,2,1,0:T(8,128)(2,1)} %all_to_all.40.refs_0_), channel_id=1, source_target_pairs={{0,16},{16,0},{1,17},{17,1},{2,18},{18,2},{3,19},{19,3},{4,20},{20... | collective-permute-start | bytes 6291464 | tf_op jit(solution)/shard_map/ppermute | solution.py:209
  197.9 1.3 copy-start.9
  199.3 107.4 %copy-start.4 = (bf16[16,16,32,128]{3,2,1,0:T(8,128)(2,1)}, bf16[16,16,32,128]{3,2,1,0:T(8,128)(2,1)S(1)}, u32[]{:S(2)}) copy-start(bf16[16,16,32,128]{3,2,1,0:T(8,128)(2,1)S(1)} %all-to-all-done.refs_0_) | copy-start | bytes 6291460
  199.3 55.0 %all-to-all-start.5 = ((bf16[16,16,32,128]{3,2,1,0:T(8,128)(2,1)}), bf16[16,16,32,128]{3,2,1,0:T(8,128)(2,1)}, u32[]{:S(2)}, u32[]{:S(2)}) async-start(bf16[16,16,32,128]{3,2,1,0:T(8,128)(2,1)} %bitcast.18), calls=%async_computation.5 | async-start | bytes 4194304 | tf_op jit(solution)/shard_map/all_to_all | solution.py:203
  205.0 47.9 %collective-permute-start = (bf16[16,16,32,128]{3,2,1,0:T(8,128)(2,1)S(1)}, bf16[16,16,32,128]{3,2,1,0:T(8,128)(2,1)S(1)}, u32[]{:S(2)}, u32[]{:S(2)}) collective-permute-start(bf16[16,16,32,128]{3,2,1,0:T(8,128)(2,1)S(1)} %all-to-all-done.refs_0_), channel_id=1, source_target_pairs={{0,16},{16,0},{1,17},{17,1},{2,18},{18,2},{3,19},{19,3},{4,20},{20... | collective-permute-start | bytes 6291464 | tf_op jit(solution)/shard_map/ppermute | solution.py:209
  252.9 1.3 copy-start.6
  254.3 54.0 %all-to-all-start.1 = ((bf16[16,16,32,128]{3,2,1,0:T(8,128)(2,1)}), bf16[16,16,32,128]{3,2,1,0:T(8,128)(2,1)}, u32[]{:S(2)}, u32[]{:S(2)}) async-start(bf16[16,16,32,128]{3,2,1,0:T(8,128)(2,1)} %bitcast.16), calls=%async_computation.1 | async-start | bytes 4194304 | tf_op jit(solution)/shard_map/all_to_all | solution.py:203
  260.0 48.2 %collective-permute-start.5 = (bf16[16,16,32,128]{3,2,1,0:T(8,128)(2,1)}, bf16[16,16,32,128]{3,2,1,0:T(8,128)(2,1)}, u32[]{:S(2)}, u32[]{:S(2)}) collective-permute-start(bf16[16,16,32,128]{3,2,1,0:T(8,128)(2,1)} %all-to-all-done.5.refs_0_), channel_id=1, source_target_pairs={{0,16},{16,0},{1,17},{17,1},{2,18},{18,2},{3,19},{19,3},{4,20},{20... | collective-permute-start | bytes 6291464 | tf_op jit(solution)/shard_map/ppermute | solution.py:209
  308.2 213.4 %copy-start.3 = (s32[10]{0:T(128)S(1)}, s32[10]{0:T(128)}, u32[]{:S(2)}) copy-start(s32[10]{0:T(128)} %constant.94.clone) | copy-start | bytes 124
  308.2 214.0 %copy-start.2 = (s32[10]{0:T(128)S(1)}, s32[10]{0:T(128)}, u32[]{:S(2)}) copy-start(s32[10]{0:T(128)} %constant.95.clone) | copy-start | bytes 124
  308.3 55.4 %all-to-all-start.6 = ((bf16[16,16,32,128]{3,2,1,0:T(8,128)(2,1)}), bf16[16,16,32,128]{3,2,1,0:T(8,128)(2,1)S(1)}, u32[]{:S(2)}, u32[]{:S(2)}) async-start(bf16[16,16,32,128]{3,2,1,0:T(8,128)(2,1)} %bitcast.19), calls=%async_computation.6 | async-start | bytes 4194304 | tf_op jit(solution)/shard_map/all_to_all | solution.py:203
  314.1 48.2 %collective-permute-start.1 = (bf16[16,16,32,128]{3,2,1,0:T(8,128)(2,1)}, bf16[16,16,32,128]{3,2,1,0:T(8,128)(2,1)S(1)}, u32[]{:S(2)}, u32[]{:S(2)}) collective-permute-start(bf16[16,16,32,128]{3,2,1,0:T(8,128)(2,1)} %all-to-all-done.1.refs_0_), channel_id=1, source_target_pairs={{0,16},{16,0},{1,17},{17,1},{2,18},{18,2},{3,19},{19,3},{4,20},{20... | collective-permute-start | bytes 6291464 | tf_op jit(solution)/shard_map/ppermute | solution.py:209
  362.3 1.3 copy-start.7
  363.6 168.8 %copy-start.5 = (bf16[16,16,32,128]{3,2,1,0:T(8,128)(2,1)}, bf16[16,16,32,128]{3,2,1,0:T(8,128)(2,1)S(1)}, u32[]{:S(2)}) copy-start(bf16[16,16,32,128]{3,2,1,0:T(8,128)(2,1)S(1)} %all-to-all-done.6.refs_0_) | copy-start | bytes 6291460
  363.6 55.0 %all-to-all-start.2 = ((bf16[16,16,32,128]{3,2,1,0:T(8,128)(2,1)}), bf16[16,16,32,128]{3,2,1,0:T(8,128)(2,1)}, u32[]{:S(2)}, u32[]{:S(2)}) async-start(bf16[16,16,32,128]{3,2,1,0:T(8,128)(2,1)} %bitcast.17), calls=%async_computation.2 | async-start | bytes 4194304 | tf_op jit(solution)/shard_map/all_to_all | solution.py:203
  369.4 47.9 %collective-permute-start.6 = (bf16[16,16,32,128]{3,2,1,0:T(8,128)(2,1)S(1)}, bf16[16,16,32,128]{3,2,1,0:T(8,128)(2,1)S(1)}, u32[]{:S(2)}, u32[]{:S(2)}) collective-permute-start(bf16[16,16,32,128]{3,2,1,0:T(8,128)(2,1)S(1)} %all-to-all-done.6.refs_0_), channel_id=1, source_target_pairs={{0,16},{16,0},{1,17},{17,1},{2,18},{18,2},{3,19},{19,3},{4,20},{20... | collective-permute-start | bytes 6291464 | tf_op jit(solution)/shard_map/ppermute | solution.py:209
  417.3 1.4 copy-start.8
  418.7 54.0 %all-to-all-start.7 = ((bf16[16,16,32,128]{3,2,1,0:T(8,128)(2,1)}), bf16[16,16,32,128]{3,2,1,0:T(8,128)(2,1)}, u32[]{:S(2)}, u32[]{:S(2)}) async-start(bf16[16,16,32,128]{3,2,1,0:T(8,128)(2,1)} %bitcast.15), calls=%async_computation.7 | async-start | bytes 4194304 | tf_op jit(solution)/shard_map/all_to_all | solution.py:203
  424.4 48.2 %collective-permute-start.2 = (bf16[16,16,32,128]{3,2,1,0:T(8,128)(2,1)}, bf16[16,16,32,128]{3,2,1,0:T(8,128)(2,1)}, u32[]{:S(2)}, u32[]{:S(2)}) collective-permute-start(bf16[16,16,32,128]{3,2,1,0:T(8,128)(2,1)} %all-to-all-done.2.refs_0_), channel_id=1, source_target_pairs={{0,16},{16,0},{1,17},{17,1},{2,18},{18,2},{3,19},{19,3},{4,20},{20... | collective-permute-start | bytes 6291464 | tf_op jit(solution)/shard_map/ppermute | solution.py:209
  472.6 46.8 %all-to-all-start.3 = ((bf16[16,16,32,128]{3,2,1,0:T(8,128)(2,1)}), bf16[16,16,32,128]{3,2,1,0:T(8,128)(2,1)}, u32[]{:S(2)}, u32[]{:S(2)}) async-start(bf16[16,16,32,128]{3,2,1,0:T(8,128)(2,1)} %bitcast.14), calls=%async_computation.3 | async-start | bytes 4194304 | tf_op jit(solution)/shard_map/all_to_all | solution.py:203
  478.4 98.5 %collective-permute-start.7 = (bf16[16,16,32,128]{3,2,1,0:T(8,128)(2,1)}, bf16[16,16,32,128]{3,2,1,0:T(8,128)(2,1)}, u32[]{:S(2)}, u32[]{:S(2)}) collective-permute-start(bf16[16,16,32,128]{3,2,1,0:T(8,128)(2,1)} %all-to-all-done.7.refs_0_), channel_id=1, source_target_pairs={{0,16},{16,0},{1,17},{17,1},{2,18},{18,2},{3,19},{19,3},{4,20},{20... | collective-permute-start | bytes 6291464 | tf_op jit(solution)/shard_map/ppermute | solution.py:209
  519.4 66.4 %collective-permute-start.3 = (bf16[16,16,32,128]{3,2,1,0:T(8,128)(2,1)}, bf16[16,16,32,128]{3,2,1,0:T(8,128)(2,1)}, u32[]{:S(2)}, u32[]{:S(2)}) collective-permute-start(bf16[16,16,32,128]{3,2,1,0:T(8,128)(2,1)} %all-to-all-done.3.refs_0_), channel_id=1, source_target_pairs={{0,16},{16,0},{1,17},{17,1},{2,18},{18,2},{3,19},{19,3},{4,20},{20... | collective-permute-start | bytes 6291464 | tf_op jit(solution)/shard_map/ppermute | solution.py:209
  585.9 9.0 %copy-start.1 = (s32[10]{0:T(128)S(1)}, s32[10]{0:T(128)}, u32[]{:S(2)}) copy-start(s32[10]{0:T(128)} %param.5) | copy-start | bytes 124
